TPU v7x, 512 devices: a whole 4x4x16 slice. The times are simulated.
512 devices in a mesh: expert: 128 (over y, z, core), cuts: 4 (over x).
Axes of the slice: x: 4, y: 4, z: 16, core: 2. Of those that a mesh axis runs over, the one named last changes fastest.
Arguments:
- tokens: bfloat16 [1024, 3584], P('expert', 'cuts'), may hold values from -6 to 6
- expert_ids: int32 [1024, 8], P('expert'), may hold values from 0 to 127, all different within a row; in each aligned block of 8 rows (0 to 7, 8 to 15, ...) at most 1 rows name the same one
- gate_weight: float32 [1024, 8], P('expert'), may hold values from 0.05 to 1
- valid_count: int32 [128], P('expert'), may hold values from 6 to 8, as said below
- up_weight: bfloat16 [128, 3584, 1024], P('expert', None, 'cuts'), may hold values from -0.09375 to 0.09375
- down_weight: bfloat16 [128, 1024, 3584], P('expert', 'cuts'), may hold values from -0.1875 to 0.1875
Outputs:
- moe_output: bfloat16 [1024, 3584], P('expert', 'cuts')
Inputs may be any that keep to these rules, and one draw needn't show every extreme that they name: `expert_ids`: each row names 8 different experts; within the rows of one group (8 rows) no expert is named more than 1 times, and in some groups one expert is named exactly 1 times. `valid_count`: live tokens of each group, between three quarters of 8 (rounded down) and 8; both ends are reached in every draw.
All inputs are finite; a program needn't handle non-finite values.
Results may differ from a plain program's by a relative error of at most 0.0081.
Values may be sent and summed in bfloat16 or wider, within the bound.
No kernel may reach another device: no remote copies, remote signals or barrier semaphores. Data moves between devices by JAX's collectives and lax.ppermute only.
A program may use at most 64 MiB of HBM per device.

v0:
```python
import jax
import jax.numpy as jnp
from jax import lax
from jax.sharding import PartitionSpec as P

route_scale = 2.827


def cut_along(array, dim, size):
    before, after = (array.shape[:dim], array.shape[dim + 1 :])
    return jnp.moveaxis(array.reshape(*before, size, -1, *after), dim, 0)


def sent_and_summed(array, axis, dim):
    size = lax.axis_size(axis)
    pieces = lax.all_to_all(cut_along(array, dim, size), axis, 0, 0, tiled=True)
    return jnp.sum(pieces.astype(jnp.float32), axis=0)


def block_tables(expert_rows, gate_rows, count_here, num_experts, slot_cap):
    tok_rows = expert_rows.shape[0]
    top_rows = expert_rows.shape[1]
    pair_total = tok_rows * top_rows
    flat_ids = expert_rows.reshape(pair_total)
    live_tok = (jnp.arange(tok_rows, dtype=jnp.int32) < count_here).astype(jnp.int32)
    live_pairs = jnp.repeat(live_tok, top_rows)
    expert_hits = (flat_ids[:, None] == jnp.arange(num_experts, dtype=jnp.int32)[None, :]).astype(
        jnp.int32
    ) * live_pairs[:, None]
    earlier = jnp.cumsum(expert_hits, axis=0) - expert_hits
    slot_index = jnp.sum(earlier * expert_hits, axis=1)
    position = flat_ids * slot_cap + slot_index
    onehot = (
        position[:, None] == jnp.arange(num_experts * slot_cap, dtype=jnp.int32)[None, :]
    ).astype(jnp.float32)
    onehot = onehot * live_pairs[:, None].astype(jnp.float32)
    onehot = onehot.reshape(tok_rows, top_rows, num_experts * slot_cap)
    shares = route_scale * gate_rows / jnp.sum(gate_rows, axis=1, keepdims=True)
    select = jnp.sum(onehot, axis=1)
    mixing = jnp.einsum("tk,tkp->tp", shares, onehot, precision=lax.Precision.HIGHEST)
    return (select, mixing)


def shards(tokens, expert_ids, gate_weight, valid_count, up_weight, down_weight):
    local_experts = up_weight.shape[0]
    num_experts = local_experts * lax.axis_size("expert")
    tok_rows = expert_ids.shape[0]
    top_rows = expert_ids.shape[1]
    slot_cap = max(1, (3 * tok_rows * top_rows + 2 * num_experts - 1) // (2 * num_experts))
    select, mixing = block_tables(expert_ids, gate_weight, valid_count[0], num_experts, slot_cap)
    picker = select.T.astype(jnp.bfloat16)
    outgoing = jnp.dot(picker, tokens, preferred_element_type=jnp.float32).astype(jnp.bfloat16)
    outgoing = outgoing.reshape(num_experts, slot_cap, tokens.shape[1])
    received = lax.all_gather(
        lax.all_to_all(outgoing, "expert", split_axis=0, concat_axis=0, tiled=True),
        "cuts",
        axis=2,
        tiled=True,
    )
    sources = received.shape[0] // local_experts
    shaped = received.reshape(sources, local_experts, received.shape[1], received.shape[2])
    raised = jnp.einsum("secd,edf->secf", shaped, up_weight, preferred_element_type=jnp.float32)
    hidden = jax.nn.silu(raised).astype(jnp.bfloat16)
    lowered = jnp.einsum("secf,efd->secd", hidden, down_weight, preferred_element_type=jnp.float32)
    partial_value = lowered.reshape(received.shape[0], received.shape[1], down_weight.shape[2])
    reduced = sent_and_summed(partial_value.astype(jnp.bfloat16), "cuts", 2)
    returned = lax.all_to_all(
        reduced.astype(jnp.bfloat16), "expert", split_axis=0, concat_axis=0, tiled=True
    ).astype(reduced.dtype)
    mixed_rows = jnp.dot(
        mixing,
        returned.reshape(num_experts * slot_cap, returned.shape[2]),
        precision=lax.Precision.HIGHEST,
        preferred_element_type=jnp.float32,
    )
    return mixed_rows.astype(jnp.bfloat16)


def solution(mesh):
    return jax.shard_map(
        shards,
        mesh=mesh,
        in_specs=(
            P("expert", "cuts"),
            P("expert", None),
            P("expert", None),
            P("expert"),
            P("expert", None, "cuts"),
            P("expert", "cuts", None),
        ),
        out_specs=P("expert", "cuts"),
        check_vma=False,
    )
```

profile of v0, /device:TPU:1, one launch (start us, length us, event | category | flops | bytes accessed | tf_op | source)
XLA Modules:
  0.0 116.2 jit_solution(9336660738229291293)
XLA Ops:
  0.0 0.0 copy-start
  0.8 0.8 eq.29
  1.6 0.1 broadcast_in_dim.2
  1.6 0.1 mul.33
  1.7 0.1 fusion.28
  1.8 0.1 reduce_window_sum.11
  1.9 0.2 fusion.27
  2.1 0.1 reduce_sum.45
  2.2 0.7 add.11
  2.9 0.1 select_reduce_fusion
  3.0 1.0 fusion.4
  4.0 0.5 broadcast.29
  4.5 0.7 reduce.2
  5.2 0.2 reshape.79
  5.4 42.7 %all_to_all.15 = bf16[128,2,448]{2,1,0:T(2,128)(2,1)S(1)} all-to-all(bf16[128,2,448]{2,1,0:T(2,128)(2,1)S(1)} %reshape.79), channel_id=1, replica_groups=mesh['expert'=128,'cuts'=4] {'expert'}, dimensions={0} | all-to-all | bytes 458752 | tf_op jit(solution)/shard_map/all_to_all | solution.py:55
  48.2 0.5 reshape.80
  48.7 12.1 %all_gather.3 = bf16[128,1,3584]{2,0,1:T(8,128)(2,1)S(1)} all-gather(bf16[128,1,896]{2,0,1:T(8,128)(2,1)S(1)} %copy.14), channel_id=1, replica_groups=mesh['expert'=128,'cuts'=4] {'cuts'}, dimensions={2}, use_global_device_ids=true | all-gather | bytes 1146880 | tf_op jit(solution)/shard_map/all_gather | solution.py:54
  60.9 0.0 copy-done
  60.9 3.6 %fusion = bf16[128,1,1,3584]{3,0,2,1:T(8,128)(2,1)} fusion(bf16[1,256,3584]{2,1,0:T(8,128)(2,1)S(1)} %copy-done, bf16[1,3584,256]{2,1,0:T(8,128)(2,1)} %param.10, bf16[128,1,3584]{2,0,1:T(8,128)(2,1)S(1)} %all_gather.3), kind=kOutput, calls=%fused_computation.1 | convolution fusion | flops 470384640 | bytes 5505024 | tf_op jit(solution)/shard_map/secf,efd->secd/dot_general | solution.py:64
  64.5 1.9 %convert_element_type.63 = bf16[128,1,4,896]{3,2,0,1:T(4,128)(2,1)S(1)} reshape(bf16[128,1,1,3584]{3,0,2,1:T(8,128)(2,1)} %fusion) | data formatting | bytes 1835008 | tf_op jit(solution)/shard_map/convert_element_type | solution.py:66
  66.4 0.1 copy.25
  66.5 0.0 copy-start.1
  66.5 13.0 %all_to_all.16 = bf16[4,128,1,896]{3,1,2,0:T(8,128)(2,1)S(1)} all-to-all(bf16[4,128,1,896]{3,1,2,0:T(8,128)(2,1)S(1)} %bitcast.69), channel_id=1, replica_groups=mesh['expert'=128,'cuts'=4] {'cuts'}, dimensions={0} | all-to-all | bytes 1835008 | tf_op jit(solution)/shard_map/all_to_all | solution.py:16
  79.6 0.1 reduce_sum.47
  79.7 0.7 reduce.3
  80.4 0.9 reshape.81
  81.4 11.1 %all-to-all-start.2 = ((bf16[128,2,448]{2,1,0:T(2,128)(2,1)}), bf16[128,2,448]{2,1,0:T(2,128)(2,1)S(1)}, u32[]{:S(2)}, u32[]{:S(2)}) async-start(bf16[128,2,448]{2,1,0:T(2,128)(2,1)} %reshape.81), calls=%async_computation.2 | async-start | bytes 524288 | tf_op jit(solution)/shard_map/all_to_all | solution.py:67
  92.5 0.0 copy-done.1
  92.5 0.1 reduce_sum.43
  92.6 0.1 multiply_divide_fusion
  92.7 0.3 fusion.25
  93.0 21.9 %all-to-all-done.2 = bf16[128,2,448]{2,1,0:T(2,128)(2,1)S(1)} async-done(((bf16[128,2,448]{2,1,0:T(2,128)(2,1)}), bf16[128,2,448]{2,1,0:T(2,128)(2,1)S(1)}, u32[]{:S(2)}, u32[]{:S(2)}) %all-to-all-start.2) | async-done | bytes 229408 | tf_op jit(solution)/shard_map/all_to_all | solution.py:67
  114.9 0.5 reshape.82
  115.4 0.8 convolution_convert_fusion.2
  (2 shorter events, 0.0 us)
Async XLA Ops:
  0.0 60.9 %copy-start = (bf16[1,256,3584]{2,1,0:T(8,128)(2,1)S(1)}, bf16[1,256,3584]{2,1,0:T(8,128)(2,1)}, u32[]{:S(2)}) copy-start(bf16[1,256,3584]{2,1,0:T(8,128)(2,1)} %param.11) | copy-start | bytes 5505028
  66.5 26.0 %copy-start.1 = (f32[8,8]{1,0:T(8,128)S(1)}, f32[8,8]{1,0:T(8,128)}, u32[]{:S(2)}) copy-start(f32[8,8]{1,0:T(8,128)} %param.8) | copy-start | bytes 772
  81.4 33.5 %all-to-all-start.2 = ((bf16[128,2,448]{2,1,0:T(2,128)(2,1)}), bf16[128,2,448]{2,1,0:T(2,128)(2,1)S(1)}, u32[]{:S(2)}, u32[]{:S(2)}) async-start(bf16[128,2,448]{2,1,0:T(2,128)(2,1)} %reshape.81), calls=%async_computation.2 | async-start | bytes 524288 | tf_op jit(solution)/shard_map/all_to_all | solution.py:67
where the time goes:
time: 117 us; the launch traced here: 116 us
  blocking collectives  67.9 us (58%)
  waiting for transfers between devices  21.9 us (19%)
  starting transfers between devices  11.1 us (9%)
  local copies, waits for them, and re-layouts  5.71 us (5%)
  matrix products  5.68 us (5%)
  other arithmetic  2.95 us (3%)
    all_to_all x1, blocking collectives, shards(): lax.all_to_all(outgoing, 'expert', split_axis=0, concat_axis=0, tiled=True)  42.7 us
    all_to_all x1, waiting for transfers between devices, shards(): lax.all_to_all(reduced.astype(jnp.bfloat16), 'expert', split_axis=0, conc...  21.9 us
    all_to_all x1, blocking collectives, sent_and_summed(): pieces = lax.all_to_all(cut_along(array, dim, size), axis, 0, 0, tiled=True)  13 us
    all_gather x1, blocking collectives, shards(): lax.all_gather(lax.all_to_all(outgoing, 'expert', split_axis=0, concat_ax...  12.1 us
    all_to_all x1, starting transfers between devices, shards(): lax.all_to_all(reduced.astype(jnp.bfloat16), 'expert', split_axis=0, conc...  11.1 us
    dot_general x1, matrix products, shards(): jnp.einsum('secf,efd->secd', hidden, down_weight, preferred_element_type=...  3.63 us
  transfers between devices with their start and end apart: 1, of which 1 were waited for; matrix products, arithmetic and copies ran while one was open for 0% of the time, Pallas kernels for 0%

commit v1 on v0

v1 whole, which is shorter than its diff:
```python
import jax
import jax.numpy as jnp
from jax import lax
from jax.experimental import pallas as pl
from jax.experimental.pallas import tpu as pltpu
from jax.sharding import Mesh, PartitionSpec as P

route_scale = 2.827
Y, ZH, ZL, C, X = 4, 8, 2, 2, 4
NEAR = Y * ZL * C
F32, BF16 = jnp.float32, jnp.bfloat16
VMEM = pl.BlockSpec(memory_space=pltpu.VMEM)
SMEM = pl.BlockSpec(memory_space=pltpu.SMEM)
NOWHERE = 255.0


def pack_kernel(tok_ref, ids_ref, gate_ref, count_ref, out_ref):
    rows, top = ids_ref.shape
    width = tok_ref.shape[1]
    ids = ids_ref[...]
    gate = gate_ref[...]
    share = route_scale * gate / jnp.sum(gate, axis=1, keepdims=True)
    high = share.astype(BF16).astype(F32)
    mid = (share - high).astype(BF16).astype(F32)
    low = (share - high - mid).astype(BF16).astype(F32)
    live = lax.broadcasted_iota(jnp.int32, ids.shape, 0) < count_ref[0]
    near = (ids // (ZH * ZL * C)) * (ZL * C) + ids % (ZL * C)
    near = jnp.where(live, near, int(NOWHERE)).astype(F32)
    far = (ids // (ZL * C)) % ZH
    lane = lax.broadcasted_iota(jnp.int32, (rows, 128), 1)
    meta = jnp.zeros((rows, 128), F32)
    goes = jnp.full((rows, 128), -1, jnp.int32)
    for k in range(top):
        at = slice(k, k + 1)
        meta = jnp.where(lane == k, near[:, at], meta)
        goes = jnp.where(lane == k, far[:, at], goes)
        for piece, part in enumerate((high, mid, low)):
            meta = jnp.where(lane == (piece + 1) * top + k, part[:, at], meta)
    tokens = tok_ref[...]
    for to in range(ZH):
        out_ref[to, :, :width] = tokens
        here = jnp.where((goes == to) | (goes < 0), meta, NOWHERE)
        out_ref[to, :, width:] = here.astype(BF16)


def match_of(meta, top):
    shape = meta.shape
    column = lax.broadcasted_iota(jnp.int32, shape, 1)
    row = lax.broadcasted_iota(jnp.int32, shape, 0)
    own = (row // 8) == (column % ZH)
    expert = jnp.where(own, column // ZH, -1).astype(F32)
    return [meta[:, k : k + 1] == expert for k in range(top)]


def pick_kernel(top, in_ref, out_ref):
    width = out_ref.shape[2]
    rows = in_ref.shape[0] * in_ref.shape[1]
    meta = in_ref[:, :, width:].astype(F32).reshape(rows, 128)
    hits = match_of(meta, top)
    named = hits[0]
    for hit in hits[1:]:
        named = named | hit
    picker = jnp.where(named, 1.0, 0.0).astype(BF16)
    tokens = in_ref[:, :, :width].astype(F32).reshape(rows, width).astype(BF16)
    picked = lax.dot_general(picker, tokens, (((0,), (0,)), ((), ())), preferred_element_type=F32)
    picked = picked.astype(BF16)
    for x in range(X):
        out_ref[x] = picked


def expert_kernel(in_ref, up_ref, down_ref, out_ref):
    width = in_ref.shape[2]
    raised = None
    for x in range(X):
        term = jnp.dot(in_ref[x], up_ref[0, x * width : (x + 1) * width, :], preferred_element_type=F32)
        raised = term if raised is None else raised + term
    hidden = (raised / (1.0 + jnp.exp(-raised))).astype(BF16)
    for x in range(X):
        lowered = jnp.dot(hidden, down_ref[0, :, x * width : (x + 1) * width], preferred_element_type=F32)
        out_ref[x] = lowered.astype(BF16)


def mix_kernel(top, meta_ref, in_ref, out_ref):
    width = in_ref.shape[2]
    rows = meta_ref.shape[0] * meta_ref.shape[1]
    meta = meta_ref[:, :, width:].astype(F32).reshape(rows, 128)
    hits = match_of(meta, top)
    pieces = []
    for piece in range(3):
        weight = jnp.zeros((rows, 128), F32)
        for k in range(top):
            at = (piece + 1) * top + k
            weight = jnp.where(hits[k], meta[:, at : at + 1], weight)
        pieces.append(weight)
    mixing = jnp.concatenate(pieces, axis=0).astype(BF16)
    total = None
    for x in range(X):
        term = jnp.dot(mixing, in_ref[x], preferred_element_type=F32)
        total = term if total is None else total + term
    mixed = (total[2 * rows :] + total[rows : 2 * rows]) + total[:rows]
    out_ref[...] = mixed.astype(BF16)


def call(kernel, out_shape, specs, name, flops, bytes_accessed):
    return pl.pallas_call(
        kernel,
        out_shape=jax.ShapeDtypeStruct(out_shape, BF16),
        in_specs=specs,
        out_specs=VMEM,
        name=name,
        compiler_params=pltpu.CompilerParams(vmem_limit_bytes=16 * 1024 * 1024),
        cost_estimate=pl.CostEstimate(flops=flops, bytes_accessed=bytes_accessed, transcendentals=0),
    )


def shards(tokens, expert_ids, gate_weight, valid_count, up_weight, down_weight):
    rows, width = tokens.shape
    top = expert_ids.shape[1]
    far, near = "zh", ("x", "y", "zl", "c")
    packed = call(pack_kernel, (ZH, rows, width + 128), [VMEM, VMEM, VMEM, SMEM], "pack", 100000, 200000)(
        tokens, expert_ids, gate_weight, valid_count
    )
    got = lax.all_to_all(packed, far, 0, 0, tiled=True)
    slots = NEAR * ZH
    picked = call(lambda *refs: pick_kernel(top, *refs), (X, slots, width), [VMEM], "pick", 2 * 64 * slots * width, 1100000)(got)
    routed = lax.all_to_all(picked.reshape(X * NEAR, ZH, width), near, 0, 0, tiled=True)
    partial = call(expert_kernel, (X, slots, width), [VMEM] * 3, "expert", 4 * slots * X * width * up_weight.shape[2], 5000000)(
        routed.reshape(X, slots, width), up_weight, down_weight
    )
    back = lax.all_to_all(partial.reshape(X * NEAR, ZH, width), near, 0, 0, tiled=True)
    mixed = call(lambda *refs: mix_kernel(top, *refs), (ZH * rows, width), [VMEM] * 2, "mix", 2 * 192 * X * slots * width, 1100000)(
        got, back.reshape(X, slots, width)
    )
    parts = lax.all_to_all(mixed.reshape(ZH, rows, width), far, 0, 0, tiled=True)
    return jnp.sum(parts.astype(F32), axis=0).astype(BF16)


def solution(mesh):
    fine = Mesh(mesh.devices.reshape(Y, ZH, ZL, C, X), ("y", "zh", "zl", "c", "x"))
    experts = ("y", "zh", "zl", "c")
    return jax.shard_map(
        shards,
        mesh=fine,
        in_specs=(
            P(experts, "x"),
            P(experts, None),
            P(experts, None),
            P(experts),
            P(experts, None, "x"),
            P(experts, "x", None),
        ),
        out_specs=P(experts, "x"),
        check_vma=False,
    )
```

time: 117 us -> 101 us (0.86)
  blocking collectives: 67.9 us -> 93.4 us
  waiting for transfers between devices: 21.9 us -> 0 us
  starting transfers between devices: 11.1 us -> 0 us
  matrix products: 5.68 us -> 0 us
  Pallas kernels: 0 us -> 2.65 us
  other arithmetic: 2.95 us -> 0.62 us
  local copies, waits for them, and re-layouts: 5.71 us -> 3.58 us
    all_to_all x2 -> x4, blocking collectives: 55.8 us -> 93.4 us  [the longest x1 28.6 us: shards(): got = lax.all_to_all(packed, far, 0, 0, tiled=True)]
    all_to_all x1 -> x0, waiting for transfers between devices: 21.9 us -> none  [shards(): lax.all_to_all(reduced.astype(jnp.bfloat16), 'expert', split_axis=0, conc...]
    all_gather x1 -> x0, blocking collectives: 12.1 us -> none  [shards(): lax.all_gather(lax.all_to_all(outgoing, 'expert', split_axis=0, concat_ax...]
    all_to_all x1 -> x0, starting transfers between devices: 11.1 us -> none  [shards(): lax.all_to_all(reduced.astype(jnp.bfloat16), 'expert', split_axis=0, conc...]
    dot_general x4 -> x0, matrix products: 5.68 us -> none  [the longest x1 3.63 us: shards(): jnp.einsum('secf,efd->secd', hidden, down_weight, preferred_element_type=...]
    pallas_call x0 -> x4, Pallas kernels: none -> 2.65 us  [the longest x1 1.33 us: shards(): call(expert_kernel, (X, slots, width), [VMEM] * 3, 'expert', 4 * slots *...]
    convert_element_type x2 -> x0, local copies, waits for them, and re-layouts: 2.03 us -> none  [shards(): reduced = sent_and_summed(partial_value.astype(jnp.bfloat16), 'cuts', 2)]
    unnamed x8 -> x10, local copies, waits for them, and re-layouts: 2.14 us -> 3.58 us
  transfers between devices with their start and end apart: 1 -> 0, of which waited for: 1 -> 0; matrix products, arithmetic and copies ran while one was open for 0% -> 0% of each run, Pallas kernels for 0% -> 0%
where the time goes in v1:
time: 101 us
  blocking collectives  93.4 us (92%)
  local copies, waits for them, and re-layouts  3.58 us (4%)
  Pallas kernels  2.65 us (3%)
    all_to_all x1, blocking collectives, shards(): got = lax.all_to_all(packed, far, 0, 0, tiled=True)  28.6 us
    all_to_all x1, blocking collectives, shards(): lax.all_to_all(picked.reshape(X * NEAR, ZH, width), near, 0, 0, tiled=True)  28.2 us
    all_to_all x1, blocking collectives, shards(): lax.all_to_all(partial.reshape(X * NEAR, ZH, width), near, 0, 0, tiled=True)  21 us
    all_to_all x1, blocking collectives, shards(): lax.all_to_all(mixed.reshape(ZH, rows, width), far, 0, 0, tiled=True)  15.5 us
    unnamed x10, local copies, waits for them, and re-layouts  3.58 us

profile of v1, /device:TPU:1, one launch (start us, length us, event | category | flops | bytes accessed | tf_op | source)
XLA Modules:
  0.0 101.1 jit_solution(17403760968651553160)
XLA Ops:
  0.0 0.0 copy-start
  0.8 0.0 copy-start.2
  0.8 0.7 copy-done.2
  1.5 0.0 copy-start.3
  1.5 0.7 copy-done.3
  2.2 0.0 copy-start.4
  2.2 0.7 copy-done.4
  2.9 0.2 pack.1
  3.1 28.6 %all_to_all.20.refs_0_ = bf16[8,8,1024]{2,1,0:T(8,128)(2,1)S(1)} all-to-all(bf16[8,8,1024]{2,1,0:T(8,128)(2,1)S(1)} %pack.1), channel_id=1, replica_groups=mesh['y'=4,'zh'=8,'zl'=2,'c'=2,'x'=4] {'zh'}, dimensions={0} | all-to-all | bytes 262144 | tf_op jit(solution)/shard_map/all_to_all | solution.py:123
  31.7 0.4 pick.1
  32.1 28.2 %all_to_all.21 = bf16[64,8,896]{2,1,0:T(8,128)(2,1)S(1)} all-to-all(bf16[64,8,896]{2,1,0:T(8,128)(2,1)S(1)} %bitcast.6), channel_id=1, replica_groups=mesh['y'=4,'zh'=8,'zl'=2,'c'=2,'x'=4] {'x','y','zl','c'}, dimensions={0} | all-to-all | bytes 1835008 | tf_op jit(solution)/shard_map/all_to_all | solution.py:126
  60.3 0.0 copy-done
  60.3 0.0 copy-start.1
  60.3 1.5 %copy-done.1 = bf16[1,256,3584]{2,1,0:T(8,128)(2,1)S(1)} copy-done((bf16[1,256,3584]{2,1,0:T(8,128)(2,1)S(1)}, bf16[1,256,3584]{2,1,0:T(8,128)(2,1)}, u32[]{:S(2)}) %copy-start.1) | copy-done | bytes 1835032
  61.8 1.3 %expert.1 = bf16[4,128,896]{2,1,0:T(8,128)(2,1)S(1)} custom-call(bf16[4,128,896]{2,1,0:T(8,128)(2,1)S(1)} %bitcast.7, bf16[1,3584,256]{2,1,0:T(8,128)(2,1)S(1)} %copy-done, bf16[1,256,3584]{2,1,0:T(8,128)(2,1)S(1)} %copy-done.1), custom_call_target="tpu_custom_call" | custom-call | flops 469762048 | bytes 5000000 | tf_op jit(solution)/shard_map/expert/pallas_call | solution.py:127
  63.2 21.0 %all_to_all.22 = bf16[64,8,896]{2,1,0:T(8,128)(2,1)S(1)} all-to-all(bf16[64,8,896]{2,1,0:T(8,128)(2,1)S(1)} %bitcast.8), channel_id=1, replica_groups=mesh['y'=4,'zh'=8,'zl'=2,'c'=2,'x'=4] {'x','y','zl','c'}, dimensions={0} | all-to-all | bytes 1835008 | tf_op jit(solution)/shard_map/all_to_all | solution.py:130
  84.2 0.7 mix.1
  84.9 15.5 %all_to_all.23 = bf16[8,8,896]{2,1,0:T(8,128)(2,1)S(1)} all-to-all(bf16[8,8,896]{2,1,0:T(8,128)(2,1)S(1)} %bitcast.9), channel_id=1, replica_groups=mesh['y'=4,'zh'=8,'zl'=2,'c'=2,'x'=4] {'zh'}, dimensions={0} | all-to-all | bytes 229376 | tf_op jit(solution)/shard_map/all_to_all | solution.py:134
  100.4 0.6 reduce_sum.12
Async XLA Ops:
  0.0 60.3 %copy-start = (bf16[1,3584,256]{2,1,0:T(8,128)(2,1)S(1)}, bf16[1,3584,256]{2,1,0:T(8,128)(2,1)}, u32[]{:S(2)}) copy-start(bf16[1,3584,256]{2,1,0:T(8,128)(2,1)} %up_ref.1) | copy-start | bytes 5505028
  0.8 0.7 copy-start.2
  1.5 0.7 copy-start.3
  2.2 0.7 copy-start.4
  60.3 1.5 %copy-start.1 = (bf16[1,256,3584]{2,1,0:T(8,128)(2,1)S(1)}, bf16[1,256,3584]{2,1,0:T(8,128)(2,1)}, u32[]{:S(2)}) copy-start(bf16[1,256,3584]{2,1,0:T(8,128)(2,1)} %down_ref.1) | copy-start | bytes 5505028

commit v2 on v1

--- a/solution.py
+++ b/solution.py
@@ -11,10 +11,18 @@
 F32, BF16 = jnp.float32, jnp.bfloat16
 VMEM = pl.BlockSpec(memory_space=pltpu.VMEM)
 SMEM = pl.BlockSpec(memory_space=pltpu.SMEM)
+HBM = pl.BlockSpec(memory_space=pltpu.HBM)
 NOWHERE = 255.0
+ZH_OF = (0, 4, 2, 6, 1, 5, 3, 7)
 
 
-def pack_kernel(tok_ref, ids_ref, gate_ref, count_ref, out_ref):
+def pack_kernel(tok_hbm, ids_hbm, gate_hbm, count_ref, out_ref, tok_ref, ids_ref, gate_ref, sems):
+    pairs = ((ids_hbm, ids_ref), (gate_hbm, gate_ref), (tok_hbm, tok_ref))
+    copies = [pltpu.make_async_copy(src, dst, sems.at[i]) for i, (src, dst) in enumerate(pairs)]
+    for copy in copies:
+        copy.start()
+    for copy in copies[:2]:
+        copy.wait()
     rows, top = ids_ref.shape
     width = tok_ref.shape[1]
     ids = ids_ref[...]
@@ -36,11 +44,13 @@
         goes = jnp.where(lane == k, far[:, at], goes)
         for piece, part in enumerate((high, mid, low)):
             meta = jnp.where(lane == (piece + 1) * top + k, part[:, at], meta)
+    for to in range(ZH):
+        here = jnp.where((goes == ZH_OF[to]) | (goes < 0), meta, NOWHERE)
+        out_ref[to, :, width:] = here.astype(BF16)
+    copies[2].wait()
     tokens = tok_ref[...]
     for to in range(ZH):
         out_ref[to, :, :width] = tokens
-        here = jnp.where((goes == to) | (goes < 0), meta, NOWHERE)
-        out_ref[to, :, width:] = here.astype(BF16)
 
 
 def match_of(meta, top):
@@ -101,43 +111,67 @@
     out_ref[...] = mixed.astype(BF16)
 
 
-def call(kernel, out_shape, specs, name, flops, bytes_accessed):
+def call(kernel, out_shape, specs, name, flops, bytes_accessed, scratch=()):
     return pl.pallas_call(
         kernel,
         out_shape=jax.ShapeDtypeStruct(out_shape, BF16),
         in_specs=specs,
         out_specs=VMEM,
+        scratch_shapes=list(scratch),
         name=name,
         compiler_params=pltpu.CompilerParams(vmem_limit_bytes=16 * 1024 * 1024),
         cost_estimate=pl.CostEstimate(flops=flops, bytes_accessed=bytes_accessed, transcendentals=0),
     )
 
 
+def in_hbm(array):
+    return pltpu.with_memory_space_constraint(array, pltpu.HBM)
+
+
 def shards(tokens, expert_ids, gate_weight, valid_count, up_weight, down_weight):
     rows, width = tokens.shape
     top = expert_ids.shape[1]
-    far, near = "zh", ("x", "y", "zl", "c")
-    packed = call(pack_kernel, (ZH, rows, width + 128), [VMEM, VMEM, VMEM, SMEM], "pack", 100000, 200000)(
-        tokens, expert_ids, gate_weight, valid_count
-    )
+    hidden = up_weight.shape[2]
+    far, near = ("zd", "zb", "za"), ("x", "y", "zl", "c")
+    slots = NEAR * ZH
+    packed = call(
+        pack_kernel,
+        (ZH, rows, width + 128),
+        [HBM] * 3 + [SMEM],
+        "pack",
+        100000,
+        200000,
+        [
+            pltpu.VMEM(tokens.shape, BF16),
+            pltpu.VMEM(expert_ids.shape, jnp.int32),
+            pltpu.VMEM(gate_weight.shape, F32),
+            pltpu.SemaphoreType.DMA((3,)),
+        ],
+    )(in_hbm(tokens), in_hbm(expert_ids), in_hbm(gate_weight), valid_count)
     got = lax.all_to_all(packed, far, 0, 0, tiled=True)
-    slots = NEAR * ZH
-    picked = call(lambda *refs: pick_kernel(top, *refs), (X, slots, width), [VMEM], "pick", 2 * 64 * slots * width, 1100000)(got)
+    picked = call(
+        lambda *refs: pick_kernel(top, *refs), (X, slots, width), [VMEM], "pick", 4 * 10**9, 1100000
+    )(got)
     routed = lax.all_to_all(picked.reshape(X * NEAR, ZH, width), near, 0, 0, tiled=True)
-    partial = call(expert_kernel, (X, slots, width), [VMEM] * 3, "expert", 4 * slots * X * width * up_weight.shape[2], 5000000)(
-        routed.reshape(X, slots, width), up_weight, down_weight
-    )
+    partial = call(
+        expert_kernel,
+        (X, slots, width),
+        [VMEM] * 3,
+        "expert",
+        4 * slots * X * width * hidden,
+        5000000,
+    )(routed.reshape(X, slots, width), up_weight, down_weight)
     back = lax.all_to_all(partial.reshape(X * NEAR, ZH, width), near, 0, 0, tiled=True)
-    mixed = call(lambda *refs: mix_kernel(top, *refs), (ZH * rows, width), [VMEM] * 2, "mix", 2 * 192 * X * slots * width, 1100000)(
-        got, back.reshape(X, slots, width)
-    )
+    mixed = call(
+        lambda *refs: mix_kernel(top, *refs), (ZH * rows, width), [VMEM] * 2, "mix", 2 * 192 * X * slots * width, 1100000
+    )(got, back.reshape(X, slots, width))
     parts = lax.all_to_all(mixed.reshape(ZH, rows, width), far, 0, 0, tiled=True)
     return jnp.sum(parts.astype(F32), axis=0).astype(BF16)
 
 
 def solution(mesh):
-    fine = Mesh(mesh.devices.reshape(Y, ZH, ZL, C, X), ("y", "zh", "zl", "c", "x"))
-    experts = ("y", "zh", "zl", "c")
+    fine = Mesh(mesh.devices.reshape(Y, 2, 2, 2, ZL, C, X), ("y", "za", "zb", "zd", "zl", "c", "x"))
+    experts = ("y", "za", "zb", "zd", "zl", "c")
     return jax.shard_map(
         shards,
         mesh=fine,

time: 101 us -> 96.5 us (0.955)
  local copies, waits for them, and re-layouts: 3.58 us -> 0.01 us
  blocking collectives: 93.4 us -> 91.5 us
    unnamed x10 -> x4, local copies, waits for them, and re-layouts: 3.58 us -> 0.01 us
    all_to_all x1, blocking collectives: 28.6 us -> 27.1 us  [shards(): got = lax.all_to_all(packed, far, 0, 0, tiled=True)]
where the time goes in v2:
time: 96.5 us; the launch traced here: 96.2 us
  blocking collectives  91.5 us (95%)
  Pallas kernels  3.4 us (4%)
    all_to_all x1, blocking collectives, shards(): lax.all_to_all(picked.reshape(X * NEAR, ZH, width), near, 0, 0, tiled=True)  28.5 us
    all_to_all x1, blocking collectives, shards(): got = lax.all_to_all(packed, far, 0, 0, tiled=True)  27.1 us
    all_to_all x1, blocking collectives, shards(): lax.all_to_all(partial.reshape(X * NEAR, ZH, width), near, 0, 0, tiled=True)  21 us
    all_to_all x1, blocking collectives, shards(): lax.all_to_all(mixed.reshape(ZH, rows, width), far, 0, 0, tiled=True)  14.9 us

profile of v2, /device:TPU:1, one launch (start us, length us, event | category | flops | bytes accessed | tf_op | source)
XLA Modules:
  0.0 96.2 jit_solution(2903889882259625432)
XLA Ops:
  0.7 0.9 pack.1
  1.6 27.1 %all_to_all.20.refs_0_ = bf16[8,8,1024]{2,1,0:T(8,128)(2,1)S(1)} all-to-all(bf16[8,8,1024]{2,1,0:T(8,128)(2,1)S(1)} %pack.1), channel_id=1, replica_groups=mesh['y'=4,'za'=2,'zb'=2,'zd'=2,'zl'=2,'c'=2,'x'=4] {'zd','zb','za'}, dimensions={0} | all-to-all | bytes 262144 | tf_op jit(solution)/shard_map/all_to_all | solution.py:151
  28.7 0.0 copy-start.1
  28.7 0.4 pick.1
  29.1 0.0 copy-start
  29.1 28.5 %all_to_all.21 = bf16[64,8,896]{2,1,0:T(8,128)(2,1)S(1)} all-to-all(bf16[64,8,896]{2,1,0:T(8,128)(2,1)S(1)} %bitcast.8), channel_id=1, replica_groups=mesh['y'=4,'za'=2,'zb'=2,'zd'=2,'zl'=2,'c'=2,'x'=4] {'x','y','zl','c'}, dimensions={0} | all-to-all | bytes 1835008 | tf_op jit(solution)/shard_map/all_to_all | solution.py:155
  57.6 0.0 copy-done.1
  57.6 0.0 copy-done
  57.6 1.3 %expert.1 = bf16[4,128,896]{2,1,0:T(8,128)(2,1)S(1)} custom-call(bf16[4,128,896]{2,1,0:T(8,128)(2,1)S(1)} %bitcast.6, bf16[1,3584,256]{2,1,0:T(8,128)(2,1)S(1)} %copy-done, bf16[1,256,3584]{2,1,0:T(8,128)(2,1)S(1)} %copy-done.1), custom_call_target="tpu_custom_call" | custom-call | flops 469762048 | bytes 5000000 | tf_op jit(solution)/shard_map/expert/pallas_call | solution.py:156
  58.9 21.0 %all_to_all.22 = bf16[64,8,896]{2,1,0:T(8,128)(2,1)S(1)} all-to-all(bf16[64,8,896]{2,1,0:T(8,128)(2,1)S(1)} %bitcast.7), channel_id=1, replica_groups=mesh['y'=4,'za'=2,'zb'=2,'zd'=2,'zl'=2,'c'=2,'x'=4] {'x','y','zl','c'}, dimensions={0} | all-to-all | bytes 1835008 | tf_op jit(solution)/shard_map/all_to_all | solution.py:164
  79.9 0.7 mix.1
  80.7 14.9 %all_to_all.23 = bf16[8,8,896]{2,1,0:T(8,128)(2,1)S(1)} all-to-all(bf16[8,8,896]{2,1,0:T(8,128)(2,1)S(1)} %bitcast.9), channel_id=1, replica_groups=mesh['y'=4,'za'=2,'zb'=2,'zd'=2,'zl'=2,'c'=2,'x'=4] {'zd','zb','za'}, dimensions={0} | all-to-all | bytes 229376 | tf_op jit(solution)/shard_map/all_to_all | solution.py:168
  95.6 0.6 reduce_sum.12
Async XLA Ops:
  28.7 28.9 %copy-start.1 = (bf16[1,256,3584]{2,1,0:T(8,128)(2,1)S(1)}, bf16[1,256,3584]{2,1,0:T(8,128)(2,1)}, u32[]{:S(2)}) copy-start(bf16[1,256,3584]{2,1,0:T(8,128)(2,1)} %down_ref.1) | copy-start | bytes 5505028
  29.1 28.5 %copy-start = (bf16[1,3584,256]{2,1,0:T(8,128)(2,1)S(1)}, bf16[1,3584,256]{2,1,0:T(8,128)(2,1)}, u32[]{:S(2)}) copy-start(bf16[1,3584,256]{2,1,0:T(8,128)(2,1)} %up_ref.1) | copy-start | bytes 5505028

commit v3 on v2

v3 whole, which is shorter than its diff:
```python
import jax
import jax.numpy as jnp
from jax import lax
from jax.experimental import pallas as pl
from jax.experimental.pallas import tpu as pltpu
from jax.sharding import Mesh, PartitionSpec as P

route_scale = 2.827
Y, ZH, ZL, C, X = 4, 8, 2, 2, 4
F32, BF16 = jnp.float32, jnp.bfloat16
VMEM = pl.BlockSpec(memory_space=pltpu.VMEM)
SMEM = pl.BlockSpec(memory_space=pltpu.SMEM)
HBM = pl.BlockSpec(memory_space=pltpu.HBM)
NOWHERE = 255.0
ZH_OF = (0, 4, 2, 6, 1, 5, 3, 7)


def pack_kernel(tok_hbm, ids_hbm, gate_hbm, count_ref, out_ref, tok_ref, ids_ref, gate_ref, sems):
    pairs = ((ids_hbm, ids_ref), (gate_hbm, gate_ref), (tok_hbm, tok_ref))
    copies = [pltpu.make_async_copy(src, dst, sems.at[i]) for i, (src, dst) in enumerate(pairs)]
    for copy in copies:
        copy.start()
    for copy in copies[:2]:
        copy.wait()
    rows, top = ids_ref.shape
    width = tok_ref.shape[1]
    ids = ids_ref[...]
    gate = gate_ref[...]
    share = route_scale * gate / jnp.sum(gate, axis=1, keepdims=True)
    high = share.astype(BF16).astype(F32)
    mid = (share - high).astype(BF16).astype(F32)
    low = (share - high - mid).astype(BF16).astype(F32)
    live = lax.broadcasted_iota(jnp.int32, ids.shape, 0) < count_ref[0]
    names = jnp.where(live, ids, int(NOWHERE)).astype(F32)
    lane = lax.broadcasted_iota(jnp.int32, (rows, 128), 1)
    meta = jnp.zeros((rows, 128), F32)
    for k in range(top):
        at = slice(k, k + 1)
        for piece, part in enumerate((names, high, mid, low)):
            meta = jnp.where(lane == piece * top + k, part[:, at], meta)
    out_ref[:, width:] = meta.astype(BF16)
    copies[2].wait()
    out_ref[:, :width] = tok_ref[...]


def pick_kernel(top, in_ref, out_ref):
    width = out_ref.shape[2]
    rows = ZH * C * in_ref.shape[2]
    meta = in_ref[:, :, :, width:].astype(F32).reshape(rows, 128)
    column = lax.broadcasted_iota(jnp.int32, (rows, 128), 1)
    row = lax.broadcasted_iota(jnp.int32, (rows, 128), 0)
    own = (row // (8 * C) == column % ZH) & ((row // 8) % C == (column // ZH) % C)
    near = column // (ZH * C)
    expert = ((near // ZL) * ZH + lax.axis_index(("za", "zb", "zd"))) * (ZL * C) + (near % ZL) * C + lax.axis_index("c")
    expert = jnp.where(own, expert, -1).astype(F32)
    named = meta[:, 0:1] == expert
    for k in range(1, top):
        named = named | (meta[:, k : k + 1] == expert)
    picker = jnp.where(named, 1.0, 0.0).astype(BF16)
    tokens = in_ref[:, :, :, :width].astype(F32).reshape(rows, width).astype(BF16)
    picked = lax.dot_general(picker, tokens, (((0,), (0,)), ((), ())), preferred_element_type=F32)
    picked = picked.astype(BF16)
    for x in range(X):
        out_ref[x] = picked


def mixing_of(top, meta):
    column = lax.broadcasted_iota(jnp.int32, meta.shape, 1)
    row = lax.broadcasted_iota(jnp.int32, meta.shape, 0)
    near = column // ZH
    expert = ((near // (ZL * C)) * ZH + lax.axis_index(("za", "zb", "zd"))) * (ZL * C) + near % (ZL * C)
    expert = jnp.where(row // 8 == column % ZH, expert, -1).astype(F32)
    hits = [meta[:, k : k + 1] == expert for k in range(top)]
    pieces = []
    for piece in range(3):
        weight = jnp.zeros(meta.shape, F32)
        for k in range(top):
            at = (piece + 1) * top + k
            weight = jnp.where(hits[k], meta[:, at : at + 1], weight)
        pieces.append(weight.astype(BF16))
    return pieces


def expert_kernel(top, in_ref, up_ref, down_ref, meta_ref, out_ref, mixing_ref):
    width = in_ref.shape[2]
    raised = None
    for x in range(X):
        term = jnp.dot(in_ref[x], up_ref[0, x * width : (x + 1) * width, :], preferred_element_type=F32)
        raised = term if raised is None else raised + term
    rows = ZH * meta_ref.shape[2]
    meta = meta_ref[:, lax.axis_index("c"), :, width:].astype(F32).reshape(rows, 128)
    for piece, weight in enumerate(mixing_of(top, meta)):
        mixing_ref[piece * rows : (piece + 1) * rows] = weight
    hidden = (raised / (1.0 + jnp.exp(-raised))).astype(BF16)
    for x in range(X):
        lowered = jnp.dot(hidden, down_ref[0, :, x * width : (x + 1) * width], preferred_element_type=F32)
        out_ref[x] = lowered.astype(BF16)


def mix_kernel(mixing_ref, in_ref, out_ref):
    rows = mixing_ref.shape[0] // 3
    total = None
    for x in range(X):
        term = jnp.dot(mixing_ref[...], in_ref[x], preferred_element_type=F32)
        total = term if total is None else total + term
    mixed = (total[2 * rows :] + total[rows : 2 * rows]) + total[:rows]
    for to in range(ZH):
        out_ref[to] = mixed[ZH_OF[to] * 8 : ZH_OF[to] * 8 + 8].astype(BF16)


def call(kernel, out_shape, specs, name, flops, bytes_accessed, scratch=()):
    return pl.pallas_call(
        kernel,
        out_shape=[jax.ShapeDtypeStruct(shape, BF16) for shape in out_shape],
        in_specs=specs,
        out_specs=[VMEM] * len(out_shape),
        scratch_shapes=list(scratch),
        name=name,
        compiler_params=pltpu.CompilerParams(vmem_limit_bytes=16 * 1024 * 1024),
        cost_estimate=pl.CostEstimate(flops=flops, bytes_accessed=bytes_accessed, transcendentals=0),
    )


def in_hbm(array):
    return pltpu.with_memory_space_constraint(array, pltpu.HBM)


def shards(tokens, expert_ids, gate_weight, valid_count, up_weight, down_weight):
    rows, width = tokens.shape
    top = expert_ids.shape[1]
    hidden = up_weight.shape[2]
    far, near = ("zd", "zb", "za"), ("x", "y", "zl")
    slots = Y * ZL * C * ZH
    (packed,) = call(
        pack_kernel,
        [(rows, width + 128)],
        [HBM] * 3 + [SMEM],
        "pack",
        100000,
        200000,
        [
            pltpu.VMEM(tokens.shape, BF16),
            pltpu.VMEM(expert_ids.shape, jnp.int32),
            pltpu.VMEM(gate_weight.shape, F32),
            pltpu.SemaphoreType.DMA((3,)),
        ],
    )(in_hbm(tokens), in_hbm(expert_ids), in_hbm(gate_weight), valid_count)
    got = lax.all_gather(packed, ("za", "zb", "zd", "c"), axis=0, tiled=False).reshape(ZH, C, rows, width + 128)
    (picked,) = call(lambda *refs: pick_kernel(top, *refs), [(X, slots, width)], [VMEM], "pick", 4 * 10**9, 1100000)(got)
    routed = lax.all_to_all(picked.reshape(X * Y * ZL, C * ZH, width), near, 0, 0, tiled=True)
    partial, mixing = call(
        lambda *refs: expert_kernel(top, *refs),
        [(X, slots, width), (3 * ZH * rows, slots)],
        [VMEM] * 4,
        "expert",
        4 * slots * X * width * hidden,
        5000000,
    )(routed.reshape(X, slots, width), up_weight, down_weight, got)
    back = lax.all_to_all(partial.reshape(X * Y * ZL * C, ZH, width), near + ("c",), 0, 0, tiled=True)
    (mixed,) = call(mix_kernel, [(ZH, rows, width)], [VMEM] * 2, "mix", 6 * ZH * rows * X * slots * width, 1100000)(
        mixing, back.reshape(X, slots, width)
    )
    parts = lax.all_to_all(mixed, far, 0, 0, tiled=True)
    return jnp.sum(parts.astype(F32), axis=0).astype(BF16)


def solution(mesh):
    fine = Mesh(mesh.devices.reshape(Y, 2, 2, 2, ZL, C, X), ("y", "za", "zb", "zd", "zl", "c", "x"))
    experts = ("y", "za", "zb", "zd", "zl", "c")
    return jax.shard_map(
        shards,
        mesh=fine,
        in_specs=(
            P(experts, "x"),
            P(experts, None),
            P(experts, None),
            P(experts),
            P(experts, None, "x"),
            P(experts, "x", None),
        ),
        out_specs=P(experts, "x"),
        check_vma=False,
    )
```

time: 96.5 us -> 95.6 us (level)
    all_to_all x4 -> x3, blocking collectives: 91.5 us -> 62.9 us  [the longest x1 23.3 us: shards(): lax.all_to_all(picked.reshape(X * Y * ZL, C * ZH, width), near, 0, 0, til...]
    all_gather x0 -> x1, blocking collectives: none -> 27.9 us  [shards(): lax.all_gather(packed, ('za', 'zb', 'zd', 'c'), axis=0, tiled=False)]
where the time goes in v3:
time: 95.6 us; the launch traced here: 95.4 us
  blocking collectives  90.8 us (95%)
  Pallas kernels  3.21 us (3%)
    all_gather x1, blocking collectives, shards(): lax.all_gather(packed, ('za', 'zb', 'zd', 'c'), axis=0, tiled=False)  27.9 us
    all_to_all x1, blocking collectives, shards(): lax.all_to_all(picked.reshape(X * Y * ZL, C * ZH, width), near, 0, 0, til...  23.3 us
    all_to_all x1, blocking collectives, shards(): lax.all_to_all(partial.reshape(X * Y * ZL * C, ZH, width), near + ('c',),...  21.9 us
    all_to_all x1, blocking collectives, shards(): parts = lax.all_to_all(mixed, far, 0, 0, tiled=True)  17.7 us

profile of v3, /device:TPU:1, one launch (start us, length us, event | category | flops | bytes accessed | tf_op | source)
XLA Modules:
  0.0 95.4 jit_solution(8266838405091409610)
XLA Ops:
  0.7 0.9 pack.1
  1.6 27.9 %all-gather = bf16[128,1024]{1,0:T(8,128)(2,1)S(1)} all-gather(bf16[8,1024]{1,0:T(8,128)(2,1)S(1)} %pack.1), channel_id=2, replica_groups=mesh['y'=4,'za'=2,'zb'=2,'zd'=2,'zl'=2,'c'=2,'x'=4] {'za','zb','zd','c'}, dimensions={0}, use_global_device_ids=true | all-gather | bytes 278528 | tf_op jit(solution)/shard_map/all_gather | solution.py:148
  29.5 0.0 copy-start.1
  29.5 0.4 pick.1
  29.9 0.0 copy-start
  29.9 23.3 %all_to_all.15 = bf16[32,16,896]{2,1,0:T(8,128)(2,1)S(1)} all-to-all(bf16[32,16,896]{2,1,0:T(8,128)(2,1)S(1)} %bitcast.10), channel_id=1, replica_groups=mesh['y'=4,'za'=2,'zb'=2,'zd'=2,'zl'=2,'c'=2,'x'=4] {'x','y','zl'}, dimensions={0} | all-to-all | bytes 1835008 | tf_op jit(solution)/shard_map/all_to_all | solution.py:150
  53.2 0.0 copy-done.1
  53.2 0.0 copy-done
  53.2 1.4 %expert.1 = (bf16[4,128,896]{2,1,0:T(8,128)(2,1)S(1)}, bf16[192,128]{1,0:T(8,128)(2,1)S(1)}) custom-call(bf16[4,128,896]{2,1,0:T(8,128)(2,1)S(1)} %bitcast.5, bf16[1,3584,256]{2,1,0:T(8,128)(2,1)S(1)} %copy-done, bf16[1,256,3584]{2,1,0:T(8,128)(2,1)S(1)} %copy-done.1, bf16[8,2,8,1024]{3,2,1,0:T(8,128)(2,1)S(1)} %bitcast.8), custom_call_target="tpu_custom_call" | custom-call | flops 469762048 | bytes 5000000 | tf_op jit(solution)/shard_map/expert/pallas_call | solution.py:151
  54.6 21.9 %all_to_all.16 = bf16[64,8,896]{2,1,0:T(8,128)(2,1)S(1)} all-to-all(bf16[64,8,896]{2,1,0:T(8,128)(2,1)S(1)} %bitcast.9), channel_id=1, replica_groups=mesh['y'=4,'za'=2,'zb'=2,'zd'=2,'zl'=2,'c'=2,'x'=4] {'x','y','zl','c'}, dimensions={0} | all-to-all | bytes 1835008 | tf_op jit(solution)/shard_map/all_to_all | solution.py:159
  76.5 0.5 mix.1
  77.0 17.7 %all_to_all.17 = bf16[8,8,896]{2,1,0:T(8,128)(2,1)S(1)} all-to-all(bf16[8,8,896]{2,1,0:T(8,128)(2,1)S(1)} %mix.1), channel_id=1, replica_groups=mesh['y'=4,'za'=2,'zb'=2,'zd'=2,'zl'=2,'c'=2,'x'=4] {'zd','zb','za'}, dimensions={0} | all-to-all | bytes 229376 | tf_op jit(solution)/shard_map/all_to_all | solution.py:163
  94.7 0.6 reduce_sum.12
Async XLA Ops:
  29.5 23.7 %copy-start.1 = (bf16[1,256,3584]{2,1,0:T(8,128)(2,1)S(1)}, bf16[1,256,3584]{2,1,0:T(8,128)(2,1)}, u32[]{:S(2)}) copy-start(bf16[1,256,3584]{2,1,0:T(8,128)(2,1)} %refs_2_.1) | copy-start | bytes 5505028
  29.9 23.3 %copy-start = (bf16[1,3584,256]{2,1,0:T(8,128)(2,1)S(1)}, bf16[1,3584,256]{2,1,0:T(8,128)(2,1)}, u32[]{:S(2)}) copy-start(bf16[1,3584,256]{2,1,0:T(8,128)(2,1)} %refs_1_.1) | copy-start | bytes 5505028

commit v4 on v3

--- a/solution.py
+++ b/solution.py
@@ -26,10 +26,9 @@
     width = tok_ref.shape[1]
     ids = ids_ref[...]
     gate = gate_ref[...]
-    share = route_scale * gate / jnp.sum(gate, axis=1, keepdims=True)
-    high = share.astype(BF16).astype(F32)
-    mid = (share - high).astype(BF16).astype(F32)
-    low = (share - high - mid).astype(BF16).astype(F32)
+    high = gate.astype(BF16).astype(F32)
+    mid = (gate - high).astype(BF16).astype(F32)
+    low = (gate - high - mid).astype(BF16).astype(F32)
     live = lax.broadcasted_iota(jnp.int32, ids.shape, 0) < count_ref[0]
     names = jnp.where(live, ids, int(NOWHERE)).astype(F32)
     lane = lax.broadcasted_iota(jnp.int32, (rows, 128), 1)
@@ -71,14 +70,18 @@
     expert = ((near // (ZL * C)) * ZH + lax.axis_index(("za", "zb", "zd"))) * (ZL * C) + near % (ZL * C)
     expert = jnp.where(row // 8 == column % ZH, expert, -1).astype(F32)
     hits = [meta[:, k : k + 1] == expert for k in range(top)]
-    pieces = []
-    for piece in range(3):
-        weight = jnp.zeros(meta.shape, F32)
-        for k in range(top):
-            at = (piece + 1) * top + k
-            weight = jnp.where(hits[k], meta[:, at : at + 1], weight)
-        pieces.append(weight.astype(BF16))
-    return pieces
+    total = jnp.zeros((meta.shape[0], 1), F32)
+    weight = jnp.zeros(meta.shape, F32)
+    for k in range(top):
+        high, mid, low = (meta[:, (piece + 1) * top + k : (piece + 1) * top + k + 1] for piece in range(3))
+        gate = (high + mid) + low
+        total = total + gate
+        weight = jnp.where(hits[k], gate, weight)
+    share = route_scale * weight / total
+    high = share.astype(BF16)
+    mid = (share - high.astype(F32)).astype(BF16)
+    low = (share - high.astype(F32) - mid.astype(F32)).astype(BF16)
+    return [high, mid, low]
 
 
 def expert_kernel(top, in_ref, up_ref, down_ref, meta_ref, out_ref, mixing_ref):

time: 95.6 us -> 95.5 us (level)
  no operation moved by 1% of the time
where the time goes in v4:
time: 95.5 us; the launch traced here: 95.2 us
  blocking collectives  90.8 us (95%)
  Pallas kernels  3.09 us (3%)
    all_gather x1, blocking collectives, shards(): lax.all_gather(packed, ('za', 'zb', 'zd', 'c'), axis=0, tiled=False)  27.9 us
    all_to_all x1, blocking collectives, shards(): lax.all_to_all(picked.reshape(X * Y * ZL, C * ZH, width), near, 0, 0, til...  23.3 us
    all_to_all x1, blocking collectives, shards(): lax.all_to_all(partial.reshape(X * Y * ZL * C, ZH, width), near + ('c',),...  21.9 us
    all_to_all x1, blocking collectives, shards(): parts = lax.all_to_all(mixed, far, 0, 0, tiled=True)  17.7 us

profile of v4, /device:TPU:1, one launch (start us, length us, event | category | flops | bytes accessed | tf_op | source)
XLA Modules:
  0.0 95.2 jit_solution(611576732702502690)
XLA Ops:
  0.7 0.8 pack.1
  1.5 27.9 %all-gather = bf16[128,1024]{1,0:T(8,128)(2,1)S(1)} all-gather(bf16[8,1024]{1,0:T(8,128)(2,1)S(1)} %pack.1), channel_id=2, replica_groups=mesh['y'=4,'za'=2,'zb'=2,'zd'=2,'zl'=2,'c'=2,'x'=4] {'za','zb','zd','c'}, dimensions={0}, use_global_device_ids=true | all-gather | bytes 278528 | tf_op jit(solution)/shard_map/all_gather | solution.py:151
  29.4 0.0 copy-start.1
  29.4 0.4 pick.1
  29.8 0.0 copy-start
  29.8 23.3 %all_to_all.15 = bf16[32,16,896]{2,1,0:T(8,128)(2,1)S(1)} all-to-all(bf16[32,16,896]{2,1,0:T(8,128)(2,1)S(1)} %bitcast.10), channel_id=1, replica_groups=mesh['y'=4,'za'=2,'zb'=2,'zd'=2,'zl'=2,'c'=2,'x'=4] {'x','y','zl'}, dimensions={0} | all-to-all | bytes 1835008 | tf_op jit(solution)/shard_map/all_to_all | solution.py:153
  53.1 0.0 copy-done.1
  53.1 0.0 copy-done
  53.1 1.3 %expert.1 = (bf16[4,128,896]{2,1,0:T(8,128)(2,1)S(1)}, bf16[192,128]{1,0:T(8,128)(2,1)S(1)}) custom-call(bf16[4,128,896]{2,1,0:T(8,128)(2,1)S(1)} %bitcast.5, bf16[1,3584,256]{2,1,0:T(8,128)(2,1)S(1)} %copy-done, bf16[1,256,3584]{2,1,0:T(8,128)(2,1)S(1)} %copy-done.1, bf16[8,2,8,1024]{3,2,1,0:T(8,128)(2,1)S(1)} %bitcast.8), custom_call_target="tpu_custom_call" | custom-call | flops 469762048 | bytes 5000000 | tf_op jit(solution)/shard_map/expert/pallas_call | solution.py:154
  54.5 21.9 %all_to_all.16 = bf16[64,8,896]{2,1,0:T(8,128)(2,1)S(1)} all-to-all(bf16[64,8,896]{2,1,0:T(8,128)(2,1)S(1)} %bitcast.9), channel_id=1, replica_groups=mesh['y'=4,'za'=2,'zb'=2,'zd'=2,'zl'=2,'c'=2,'x'=4] {'x','y','zl','c'}, dimensions={0} | all-to-all | bytes 1835008 | tf_op jit(solution)/shard_map/all_to_all | solution.py:162
  76.4 0.5 mix.1
  76.9 17.7 %all_to_all.17 = bf16[8,8,896]{2,1,0:T(8,128)(2,1)S(1)} all-to-all(bf16[8,8,896]{2,1,0:T(8,128)(2,1)S(1)} %mix.1), channel_id=1, replica_groups=mesh['y'=4,'za'=2,'zb'=2,'zd'=2,'zl'=2,'c'=2,'x'=4] {'zd','zb','za'}, dimensions={0} | all-to-all | bytes 229376 | tf_op jit(solution)/shard_map/all_to_all | solution.py:166
  94.6 0.6 reduce_sum.12
Async XLA Ops:
  29.4 23.7 %copy-start.1 = (bf16[1,256,3584]{2,1,0:T(8,128)(2,1)S(1)}, bf16[1,256,3584]{2,1,0:T(8,128)(2,1)}, u32[]{:S(2)}) copy-start(bf16[1,256,3584]{2,1,0:T(8,128)(2,1)} %refs_2_.1) | copy-start | bytes 5505028
  29.8 23.3 %copy-start = (bf16[1,3584,256]{2,1,0:T(8,128)(2,1)S(1)}, bf16[1,3584,256]{2,1,0:T(8,128)(2,1)}, u32[]{:S(2)}) copy-start(bf16[1,3584,256]{2,1,0:T(8,128)(2,1)} %refs_1_.1) | copy-start | bytes 5505028

commit v5 on v4

--- a/solution.py
+++ b/solution.py
@@ -102,9 +102,12 @@
 
 def mix_kernel(mixing_ref, in_ref, out_ref):
     rows = mixing_ref.shape[0] // 3
+    twice = jnp.concatenate([mixing_ref[...]] * 2, axis=1)
+    slots, width = in_ref.shape[1:]
     total = None
-    for x in range(X):
-        term = jnp.dot(mixing_ref[...], in_ref[x], preferred_element_type=F32)
+    for x in range(0, X, 2):
+        pair = in_ref[x : x + 2].reshape(2 * slots, width)
+        term = jnp.dot(twice, pair, preferred_element_type=F32)
         total = term if total is None else total + term
     mixed = (total[2 * rows :] + total[rows : 2 * rows]) + total[:rows]
     for to in range(ZH):

time: 95.5 us -> 95.4 us (level)
  no operation moved by 1% of the time
where the time goes in v5:
time: 95.4 us; the launch traced here: 95.1 us
  blocking collectives  90.8 us (95%)
  Pallas kernels  2.97 us (3%)
    all_gather x1, blocking collectives, shards(): lax.all_gather(packed, ('za', 'zb', 'zd', 'c'), axis=0, tiled=False)  27.9 us
    all_to_all x1, blocking collectives, shards(): lax.all_to_all(picked.reshape(X * Y * ZL, C * ZH, width), near, 0, 0, til...  23.3 us
    all_to_all x1, blocking collectives, shards(): lax.all_to_all(partial.reshape(X * Y * ZL * C, ZH, width), near + ('c',),...  21.9 us
    all_to_all x1, blocking collectives, shards(): parts = lax.all_to_all(mixed, far, 0, 0, tiled=True)  17.7 us

profile of v5, /device:TPU:1, one launch (start us, length us, event | category | flops | bytes accessed | tf_op | source)
XLA Modules:
  0.0 95.1 jit_solution(4603879629424264005)
XLA Ops:
  0.7 0.8 pack.1
  1.5 27.9 %all-gather = bf16[128,1024]{1,0:T(8,128)(2,1)S(1)} all-gather(bf16[8,1024]{1,0:T(8,128)(2,1)S(1)} %pack.1), channel_id=2, replica_groups=mesh['y'=4,'za'=2,'zb'=2,'zd'=2,'zl'=2,'c'=2,'x'=4] {'za','zb','zd','c'}, dimensions={0}, use_global_device_ids=true | all-gather | bytes 278528 | tf_op jit(solution)/shard_map/all_gather | solution.py:154
  29.4 0.0 copy-start.1
  29.4 0.4 pick.1
  29.8 0.0 copy-start
  29.8 23.3 %all_to_all.15 = bf16[32,16,896]{2,1,0:T(8,128)(2,1)S(1)} all-to-all(bf16[32,16,896]{2,1,0:T(8,128)(2,1)S(1)} %bitcast.10), channel_id=1, replica_groups=mesh['y'=4,'za'=2,'zb'=2,'zd'=2,'zl'=2,'c'=2,'x'=4] {'x','y','zl'}, dimensions={0} | all-to-all | bytes 1835008 | tf_op jit(solution)/shard_map/all_to_all | solution.py:156
  53.1 0.0 copy-done.1
  53.1 0.0 copy-done
  53.1 1.3 %expert.1 = (bf16[4,128,896]{2,1,0:T(8,128)(2,1)S(1)}, bf16[192,128]{1,0:T(8,128)(2,1)S(1)}) custom-call(bf16[4,128,896]{2,1,0:T(8,128)(2,1)S(1)} %bitcast.5, bf16[1,3584,256]{2,1,0:T(8,128)(2,1)S(1)} %copy-done, bf16[1,256,3584]{2,1,0:T(8,128)(2,1)S(1)} %copy-done.1, bf16[8,2,8,1024]{3,2,1,0:T(8,128)(2,1)S(1)} %bitcast.8), custom_call_target="tpu_custom_call" | custom-call | flops 469762048 | bytes 5000000 | tf_op jit(solution)/shard_map/expert/pallas_call | solution.py:157
  54.5 21.9 %all_to_all.16 = bf16[64,8,896]{2,1,0:T(8,128)(2,1)S(1)} all-to-all(bf16[64,8,896]{2,1,0:T(8,128)(2,1)S(1)} %bitcast.9), channel_id=1, replica_groups=mesh['y'=4,'za'=2,'zb'=2,'zd'=2,'zl'=2,'c'=2,'x'=4] {'x','y','zl','c'}, dimensions={0} | all-to-all | bytes 1835008 | tf_op jit(solution)/shard_map/all_to_all | solution.py:165
  76.4 0.4 mix.1
  76.8 17.7 %all_to_all.17 = bf16[8,8,896]{2,1,0:T(8,128)(2,1)S(1)} all-to-all(bf16[8,8,896]{2,1,0:T(8,128)(2,1)S(1)} %mix.1), channel_id=1, replica_groups=mesh['y'=4,'za'=2,'zb'=2,'zd'=2,'zl'=2,'c'=2,'x'=4] {'zd','zb','za'}, dimensions={0} | all-to-all | bytes 229376 | tf_op jit(solution)/shard_map/all_to_all | solution.py:169
  94.5 0.6 reduce_sum.12
Async XLA Ops:
  29.4 23.7 %copy-start.1 = (bf16[1,256,3584]{2,1,0:T(8,128)(2,1)S(1)}, bf16[1,256,3584]{2,1,0:T(8,128)(2,1)}, u32[]{:S(2)}) copy-start(bf16[1,256,3584]{2,1,0:T(8,128)(2,1)} %refs_2_.1) | copy-start | bytes 5505028
  29.8 23.3 %copy-start = (bf16[1,3584,256]{2,1,0:T(8,128)(2,1)S(1)}, bf16[1,3584,256]{2,1,0:T(8,128)(2,1)}, u32[]{:S(2)}) copy-start(bf16[1,3584,256]{2,1,0:T(8,128)(2,1)} %refs_1_.1) | copy-start | bytes 5505028

commit v6 on v4

--- a/solution.py
+++ b/solution.py
@@ -102,10 +102,9 @@
 
 def mix_kernel(mixing_ref, in_ref, out_ref):
     rows = mixing_ref.shape[0] // 3
-    total = None
-    for x in range(X):
-        term = jnp.dot(mixing_ref[...], in_ref[x], preferred_element_type=F32)
-        total = term if total is None else total + term
+    wide = jnp.concatenate([mixing_ref[...]] * X, axis=1)
+    slots, width = in_ref.shape[1:]
+    total = jnp.dot(wide, in_ref[...].reshape(X * slots, width), preferred_element_type=F32)
     mixed = (total[2 * rows :] + total[rows : 2 * rows]) + total[:rows]
     for to in range(ZH):
         out_ref[to] = mixed[ZH_OF[to] * 8 : ZH_OF[to] * 8 + 8].astype(BF16)

time: 95.5 us -> 95.4 us (level)
  no operation moved by 1% of the time
where the time goes in v6:
time: 95.4 us; the launch traced here: 95.1 us
  blocking collectives  90.8 us (95%)
  Pallas kernels  2.97 us (3%)
    all_gather x1, blocking collectives, shards(): lax.all_gather(packed, ('za', 'zb', 'zd', 'c'), axis=0, tiled=False)  27.9 us
    all_to_all x1, blocking collectives, shards(): lax.all_to_all(picked.reshape(X * Y * ZL, C * ZH, width), near, 0, 0, til...  23.3 us
    all_to_all x1, blocking collectives, shards(): lax.all_to_all(partial.reshape(X * Y * ZL * C, ZH, width), near + ('c',),...  21.9 us
    all_to_all x1, blocking collectives, shards(): parts = lax.all_to_all(mixed, far, 0, 0, tiled=True)  17.7 us

profile of v6, /device:TPU:1, one launch (start us, length us, event | category | flops | bytes accessed | tf_op | source)
XLA Modules:
  0.0 95.1 jit_solution(10674247791049113626)
XLA Ops:
  0.7 0.8 pack.1
  1.5 27.9 %all-gather = bf16[128,1024]{1,0:T(8,128)(2,1)S(1)} all-gather(bf16[8,1024]{1,0:T(8,128)(2,1)S(1)} %pack.1), channel_id=2, replica_groups=mesh['y'=4,'za'=2,'zb'=2,'zd'=2,'zl'=2,'c'=2,'x'=4] {'za','zb','zd','c'}, dimensions={0}, use_global_device_ids=true | all-gather | bytes 278528 | tf_op jit(solution)/shard_map/all_gather | solution.py:150
  29.4 0.0 copy-start.1
  29.4 0.4 pick.1
  29.8 0.0 copy-start
  29.8 23.3 %all_to_all.15 = bf16[32,16,896]{2,1,0:T(8,128)(2,1)S(1)} all-to-all(bf16[32,16,896]{2,1,0:T(8,128)(2,1)S(1)} %bitcast.10), channel_id=1, replica_groups=mesh['y'=4,'za'=2,'zb'=2,'zd'=2,'zl'=2,'c'=2,'x'=4] {'x','y','zl'}, dimensions={0} | all-to-all | bytes 1835008 | tf_op jit(solution)/shard_map/all_to_all | solution.py:152
  53.1 0.0 copy-done.1
  53.1 0.0 copy-done
  53.1 1.3 %expert.1 = (bf16[4,128,896]{2,1,0:T(8,128)(2,1)S(1)}, bf16[192,128]{1,0:T(8,128)(2,1)S(1)}) custom-call(bf16[4,128,896]{2,1,0:T(8,128)(2,1)S(1)} %bitcast.5, bf16[1,3584,256]{2,1,0:T(8,128)(2,1)S(1)} %copy-done, bf16[1,256,3584]{2,1,0:T(8,128)(2,1)S(1)} %copy-done.1, bf16[8,2,8,1024]{3,2,1,0:T(8,128)(2,1)S(1)} %bitcast.8), custom_call_target="tpu_custom_call" | custom-call | flops 469762048 | bytes 5000000 | tf_op jit(solution)/shard_map/expert/pallas_call | solution.py:153
  54.5 21.9 %all_to_all.16 = bf16[64,8,896]{2,1,0:T(8,128)(2,1)S(1)} all-to-all(bf16[64,8,896]{2,1,0:T(8,128)(2,1)S(1)} %bitcast.9), channel_id=1, replica_groups=mesh['y'=4,'za'=2,'zb'=2,'zd'=2,'zl'=2,'c'=2,'x'=4] {'x','y','zl','c'}, dimensions={0} | all-to-all | bytes 1835008 | tf_op jit(solution)/shard_map/all_to_all | solution.py:161
  76.4 0.4 mix.1
  76.8 17.7 %all_to_all.17 = bf16[8,8,896]{2,1,0:T(8,128)(2,1)S(1)} all-to-all(bf16[8,8,896]{2,1,0:T(8,128)(2,1)S(1)} %mix.1), channel_id=1, replica_groups=mesh['y'=4,'za'=2,'zb'=2,'zd'=2,'zl'=2,'c'=2,'x'=4] {'zd','zb','za'}, dimensions={0} | all-to-all | bytes 229376 | tf_op jit(solution)/shard_map/all_to_all | solution.py:165
  94.5 0.6 reduce_sum.12
Async XLA Ops:
  29.4 23.7 %copy-start.1 = (bf16[1,256,3584]{2,1,0:T(8,128)(2,1)S(1)}, bf16[1,256,3584]{2,1,0:T(8,128)(2,1)}, u32[]{:S(2)}) copy-start(bf16[1,256,3584]{2,1,0:T(8,128)(2,1)} %refs_2_.1) | copy-start | bytes 5505028
  29.8 23.3 %copy-start = (bf16[1,3584,256]{2,1,0:T(8,128)(2,1)S(1)}, bf16[1,3584,256]{2,1,0:T(8,128)(2,1)}, u32[]{:S(2)}) copy-start(bf16[1,3584,256]{2,1,0:T(8,128)(2,1)} %refs_1_.1) | copy-start | bytes 5505028
